TPU v7x, 32 devices: a whole 2x2x4 slice. The times are simulated.
32 devices in a mesh: row: 16 (over z, y, core), col: 2 (over x).
Axes of the slice: x: 2, y: 2, z: 4, core: 2. Of those that a mesh axis runs over, the one named last changes fastest.
Arguments:
- start: float32 [32768, 128], P(('row', 'col')), may hold values from -18 to 18
- couplings: bfloat16 [128, 5, 256, 256], P(('row', 'col')), may hold values from -0.15625 to 0.15625
- tile_cols: int32 [128, 5], P(('row', 'col')), may hold values from 0 to 19
- stiffness: float32 [32768], P(('row', 'col')), may hold values from 1.5 to 4
- masses: float32 [32768], P(('row', 'col')), may hold values from 0.8 to 2.5, as said below
- bounds: float32 [2], replicated, may hold values from 1.8 to 6.5, as said below
Outputs:
- basis: float32 [32768, 128], P(('row', 'col'))
- ritz: float32 [128, 128], replicated
Inputs may be any that keep to these rules, and one draw needn't show every extreme that they name: Positive masses. bounds[0] < bounds[1].
All inputs are finite; a program needn't handle non-finite values.
Results may differ from a plain program's by a relative error of at most 0.0014.
Values may be sent and summed in bfloat16 or wider, within the bound.
No kernel may reach another device: no remote copies, remote signals or barrier semaphores. Data moves between devices by JAX's collectives and lax.ppermute only.
A program may use at most 64 MiB of HBM per device.

v0:
```python
import jax
import jax.numpy as jnp
from jax import lax
from jax.sharding import PartitionSpec as P

DEGREE = 8


def with_halo(cells, sides, width):
    for axis, dim in sides:
        count = lax.axis_size(axis)
        ends = count - 1
        head = lax.slice_in_dim(cells, 0, width, axis=dim)
        tail = lax.slice_in_dim(cells, cells.shape[dim] - width, cells.shape[dim], axis=dim)
        cells = jnp.concatenate(
            [
                lax.ppermute(tail, axis, [(i, (i + 1) % count) for i in range(ends)]),
                cells,
                lax.ppermute(head, axis, [((i + 1) % count, i) for i in range(ends)]),
            ],
            axis=dim,
        )
    return cells


def matmul_high(left, right):
    return jnp.dot(left, right, precision=lax.Precision.HIGHEST, preferred_element_type=jnp.float32)


def cholesky_inverse(gram, identity):
    factor = jnp.linalg.cholesky(gram)
    return lax.linalg.triangular_solve(factor, identity, left_side=True, lower=True)


def per_device(start, couplings, tile_cols, stiffness, masses, bounds):
    rows_dev, vec_width = start.shape
    per_block = couplings.shape[0]
    tile_size = couplings.shape[2]
    node_count = rows_dev * lax.axis_size("row") * lax.axis_size("col")

    def coupled(vectors):
        rounded = vectors.astype(jnp.bfloat16)
        line = lax.all_gather(rounded[None], "col", axis=0, tiled=True)
        column_pad = with_halo(rounded[None], (("row", 0),), 1)
        here = lax.axis_index("col")
        count = lax.axis_size("col")
        left = lax.dynamic_index_in_dim(line, jnp.maximum(here - 1, 0), 0, keepdims=False)
        right = lax.dynamic_index_in_dim(line, jnp.minimum(here + 1, count - 1), 0, keepdims=False)
        left = jnp.where(here > 0, left, jnp.zeros_like(left))
        right = jnp.where(here < count - 1, right, jnp.zeros_like(right))
        sides = [rounded, column_pad[0], column_pad[2], left, right]
        stack = jnp.stack(sides).reshape(5 * per_block, tile_size, vec_width)
        picked = stack[tile_cols]
        products = jnp.einsum(
            "psab,psbk->pak", couplings, picked, preferred_element_type=jnp.float32
        )
        return products.reshape(rows_dev, vec_width)

    stiff_column = stiffness[:, None]
    inverse_mass = 1.0 / masses[:, None]

    def stiff(vectors):
        return stiff_column * vectors - coupled(vectors)

    cut_low = bounds[0]
    cut_high = bounds[1]
    center = 0.5 * (cut_high + cut_low)
    radius = 0.5 * (cut_high - cut_low)
    scale_first = -radius / center
    twice_inverse = 2.0 / scale_first
    previous = start
    current = scale_first / radius * (stiff(start) * inverse_mass - center * start)
    scale_now = scale_first
    for iteration in range(DEGREE - 1):
        scale_next = 1.0 / (twice_inverse - scale_now)
        following = (
            2.0 * scale_next / radius * (stiff(current) * inverse_mass - center * current)
            - scale_now * scale_next * previous
        )
        previous, current, scale_now = (current, following, scale_next)
    weighted = masses[:, None] / node_count
    identity = jnp.eye(vec_width, dtype=jnp.float32)
    gram_local = matmul_high(current.T, weighted * current)
    gram = lax.psum(gram_local, ("row", "col"))
    projected = lax.psum(matmul_high(current.T, stiff(current) / node_count), ("row", "col"))
    inverse = cholesky_inverse(gram, identity)
    basis = matmul_high(current, inverse.T)
    ritz = matmul_high(matmul_high(inverse, projected), inverse.T)
    return (basis, ritz)


def solution(mesh):
    return jax.shard_map(
        per_device,
        mesh=mesh,
        in_specs=(
            P(("row", "col"), None),
            P(("row", "col"), None, None, None),
            P(("row", "col"), None),
            P(("row", "col")),
            P(("row", "col")),
            P(),
        ),
        out_specs=(P(("row", "col"), None), P()),
        check_vma=False,
    )
```

profile of v0, /device:TPU:0, one launch (start us, length us, event | category | flops | bytes accessed | tf_op | source)
XLA Modules:
  0.0 429.3 jit_solution(4073234901786170040)
XLA Ops:
  18.3 8.2 %all-gather = bf16[2048,128]{1,0:T(8,128)(2,1)S(1)} all-gather(bf16[1024,128]{1,0:T(8,128)(2,1)S(1)} %get-tuple-element.17), channel_id=2, replica_groups=mesh['row'=16,'col'=2] {'col'}, dimensions={0}, use_global_device_ids=true | all-gather | bytes 786432 | tf_op jit(solution)/shard_map/all_gather | solution.py:43
  29.5 3.2 gather_fusion
  40.0 4.4 %collective-permute-start.2 = (bf16[1,1024,128]{2,1,0:T(8,128)(2,1)S(1)}, bf16[1,1024,128]{2,1,0:T(8,128)(2,1)}, u32[]{:S(2)}, u32[]{:S(2)}) collective-permute-start(bf16[1,1024,128]{2,1,0:T(8,128)(2,1)S(1)} %bitcast.273), channel_id=1, source_target_pairs={{0,2},{2,4},{4,6},{6,8},{8,10},{10,12},{12,14},{14,16},{16,18},{18... | collective-permute-start | bytes 786440 | tf_op jit(solution)/shard_map/ppermute | solution.py:17
  45.8 7.2 %all-gather.1 = bf16[2048,128]{1,0:T(8,128)(2,1)S(1)} all-gather(bf16[1024,128]{1,0:T(8,128)(2,1)S(1)} %get-tuple-element.23), channel_id=3, replica_groups=mesh['row'=16,'col'=2] {'col'}, dimensions={0}, use_global_device_ids=true | all-gather | bytes 786432 | tf_op jit(solution)/shard_map/all_gather | solution.py:43
  57.9 3.2 gather_fusion.1
  68.7 5.1 %collective-permute-start.4 = (bf16[1,1024,128]{2,1,0:T(8,128)(2,1)S(1)}, bf16[1,1024,128]{2,1,0:T(8,128)(2,1)}, u32[]{:S(2)}, u32[]{:S(2)}) collective-permute-start(bf16[1,1024,128]{2,1,0:T(8,128)(2,1)S(1)} %bitcast.269), channel_id=1, source_target_pairs={{0,2},{2,4},{4,6},{6,8},{8,10},{10,12},{12,14},{14,16},{16,18},{18... | collective-permute-start | bytes 786440 | tf_op jit(solution)/shard_map/ppermute | solution.py:17
  75.2 7.0 %all-gather.2 = bf16[2048,128]{1,0:T(8,128)(2,1)S(1)} all-gather(bf16[1024,128]{1,0:T(8,128)(2,1)S(1)} %get-tuple-element.15), channel_id=4, replica_groups=mesh['row'=16,'col'=2] {'col'}, dimensions={0}, use_global_device_ids=true | all-gather | bytes 786432 | tf_op jit(solution)/shard_map/all_gather | solution.py:43
  87.2 3.2 gather_fusion.2
  90.3 3.1 convolution_bitcast_fusion.6
  98.1 5.2 %collective-permute-start.6 = (bf16[1,1024,128]{2,1,0:T(8,128)(2,1)S(1)}, bf16[1,1024,128]{2,1,0:T(8,128)(2,1)S(1)}, u32[]{:S(2)}, u32[]{:S(2)}) collective-permute-start(bf16[1,1024,128]{2,1,0:T(8,128)(2,1)S(1)} %bitcast.275), channel_id=1, source_target_pairs={{0,2},{2,4},{4,6},{6,8},{8,10},{10,12},{12,14},{14,16},{16,18},{18... | collective-permute-start | bytes 786440 | tf_op jit(solution)/shard_map/ppermute | solution.py:17
  104.7 7.0 %all-gather.3 = bf16[2048,128]{1,0:T(8,128)(2,1)S(1)} all-gather(bf16[1024,128]{1,0:T(8,128)(2,1)S(1)} %get-tuple-element.13), channel_id=5, replica_groups=mesh['row'=16,'col'=2] {'col'}, dimensions={0}, use_global_device_ids=true | all-gather | bytes 786432 | tf_op jit(solution)/shard_map/all_gather | solution.py:43
  114.8 3.2 gather_fusion.3
  125.6 6.0 %collective-permute-start.8 = (bf16[1,1024,128]{2,1,0:T(8,128)(2,1)S(1)}, bf16[1,1024,128]{2,1,0:T(8,128)(2,1)S(1)}, u32[]{:S(2)}, u32[]{:S(2)}) collective-permute-start(bf16[1,1024,128]{2,1,0:T(8,128)(2,1)S(1)} %bitcast.277), channel_id=1, source_target_pairs={{0,2},{2,4},{4,6},{6,8},{8,10},{10,12},{12,14},{14,16},{16,18},{18... | collective-permute-start | bytes 786440 | tf_op jit(solution)/shard_map/ppermute | solution.py:17
  133.0 7.0 %all-gather.4 = bf16[2048,128]{1,0:T(8,128)(2,1)S(1)} all-gather(bf16[1024,128]{1,0:T(8,128)(2,1)S(1)} %get-tuple-element.11), channel_id=6, replica_groups=mesh['row'=16,'col'=2] {'col'}, dimensions={0}, use_global_device_ids=true | all-gather | bytes 786432 | tf_op jit(solution)/shard_map/all_gather | solution.py:43
  143.0 3.2 gather_fusion.4
  151.9 6.7 %collective-permute-start.10 = (bf16[1,1024,128]{2,1,0:T(8,128)(2,1)S(1)}, bf16[1,1024,128]{2,1,0:T(8,128)(2,1)}, u32[]{:S(2)}, u32[]{:S(2)}) collective-permute-start(bf16[1,1024,128]{2,1,0:T(8,128)(2,1)S(1)} %bitcast.279), channel_id=1, source_target_pairs={{0,2},{2,4},{4,6},{6,8},{8,10},{10,12},{12,14},{14,16},{16,18},{18... | collective-permute-start | bytes 786440 | tf_op jit(solution)/shard_map/ppermute | solution.py:17
  160.0 7.0 %all-gather.5 = bf16[2048,128]{1,0:T(8,128)(2,1)S(1)} all-gather(bf16[1024,128]{1,0:T(8,128)(2,1)S(1)} %get-tuple-element.9), channel_id=7, replica_groups=mesh['row'=16,'col'=2] {'col'}, dimensions={0}, use_global_device_ids=true | all-gather | bytes 786432 | tf_op jit(solution)/shard_map/all_gather | solution.py:43
  172.0 3.2 gather_fusion.5
  175.2 3.1 convolution_bitcast_fusion.3
  182.8 6.0 %collective-permute-start.12 = (bf16[1,1024,128]{2,1,0:T(8,128)(2,1)S(1)}, bf16[1,1024,128]{2,1,0:T(8,128)(2,1)}, u32[]{:S(2)}, u32[]{:S(2)}) collective-permute-start(bf16[1,1024,128]{2,1,0:T(8,128)(2,1)S(1)} %bitcast.281), channel_id=1, source_target_pairs={{0,2},{2,4},{4,6},{6,8},{8,10},{10,12},{12,14},{14,16},{16,18},{18... | collective-permute-start | bytes 786440 | tf_op jit(solution)/shard_map/ppermute | solution.py:17
  190.2 7.2 %all-gather.6 = bf16[2048,128]{1,0:T(8,128)(2,1)S(1)} all-gather(bf16[1024,128]{1,0:T(8,128)(2,1)S(1)} %get-tuple-element.7), channel_id=8, replica_groups=mesh['row'=16,'col'=2] {'col'}, dimensions={0}, use_global_device_ids=true | all-gather | bytes 786432 | tf_op jit(solution)/shard_map/all_gather | solution.py:43
  202.3 3.2 gather_fusion.6
  205.5 3.1 convolution_bitcast_fusion.2
  212.9 5.3 %collective-permute-start.14 = (bf16[1,1024,128]{2,1,0:T(8,128)(2,1)S(1)}, bf16[1,1024,128]{2,1,0:T(8,128)(2,1)S(1)}, u32[]{:S(2)}, u32[]{:S(2)}) collective-permute-start(bf16[1,1024,128]{2,1,0:T(8,128)(2,1)S(1)} %bitcast.267), channel_id=1, source_target_pairs={{0,2},{2,4},{4,6},{6,8},{8,10},{10,12},{12,14},{14,16},{16,18},{18... | collective-permute-start | bytes 786440 | tf_op jit(solution)/shard_map/ppermute | solution.py:17
  219.6 7.0 %all-gather.7 = bf16[2048,128]{1,0:T(8,128)(2,1)S(1)} all-gather(bf16[1024,128]{1,0:T(8,128)(2,1)S(1)} %get-tuple-element.30), channel_id=9, replica_groups=mesh['row'=16,'col'=2] {'col'}, dimensions={0}, use_global_device_ids=true | all-gather | bytes 786432 | tf_op jit(solution)/shard_map/all_gather | solution.py:43
  229.6 3.2 gather_fusion.7
  238.0 5.2 %collective-permute-start.16 = (bf16[1,1024,128]{2,1,0:T(8,128)(2,1)S(1)}, bf16[1,1024,128]{2,1,0:T(8,128)(2,1)S(1)}, u32[]{:S(2)}, u32[]{:S(2)}) collective-permute-start(bf16[1,1024,128]{2,1,0:T(8,128)(2,1)S(1)} %bitcast.265), channel_id=1, source_target_pairs={{0,2},{2,4},{4,6},{6,8},{8,10},{10,12},{12,14},{14,16},{16,18},{18... | collective-permute-start | bytes 786440 | tf_op jit(solution)/shard_map/ppermute | solution.py:17
  246.3 7.0 %all-gather.8 = bf16[2048,128]{1,0:T(8,128)(2,1)S(1)} all-gather(bf16[1024,128]{1,0:T(8,128)(2,1)S(1)} %get-tuple-element.5), channel_id=10, replica_groups=mesh['row'=16,'col'=2] {'col'}, dimensions={0}, use_global_device_ids=true | all-gather | bytes 786432 | tf_op jit(solution)/shard_map/all_gather | solution.py:43
  254.7 3.2 gather_fusion.8
  265.9 129.1 %all-reduce.3.cloned.1.call-done = (f32[128,128]{0,1:T(8,128)}, f32[128,128]{1,0:T(8,128)}) async-done(((f32[128,128]{0,1:T(8,128)}, f32[128,128]{1,0:T(8,128)}), (f32[128,128]{0,1:T(8,128)}, f32[128,128]{1,0:T(8,128)})) %all-reduce.3.cloned.1.call-update) | async-done | bytes 131088 | tf_op jit(solution)/shard_map/psum | solution.py:84
  396.9 11.7 %cholesky.17 = f32[128,128]{1,0:T(8,128)S(1)} custom-call(f32[128,128]{1,0:T(8,128)S(1)} %fusion.38), custom_call_target="Cholesky" | custom-call | tf_op jit(solution)/shard_map/jit(cholesky)/cholesky | solution.py:31
  409.9 9.8 %custom-call.6 = f32[1,128,128]{1,2,0:T(8,128)S(1)} custom-call(f32[1,128,128]{2,1,0:T(8,128)S(1)} %fusion.35), custom_call_target="InvertDiagBlocksLowerTriangular" | custom-call | tf_op jit(solution)/shard_map/triangular_solve | solution.py:32
  (121 shorter events, 114.3 us)
Async XLA Ops:
  7.2 25.6 %copy-start = (bf16[4,5,256,256]{3,2,1,0:T(8,128)(2,1)S(1)}, bf16[4,5,256,256]{3,2,1,0:T(8,128)(2,1)}, u32[]{:S(2)}) copy-start(bf16[4,5,256,256]{3,2,1,0:T(8,128)(2,1)} %param.7) | copy-start | bytes 7864324
  7.2 387.9 %all-reduce.3.cloned.1.call-start = ((), (), s32[]{:S(2)}) async-start(), calls=%async_computation | async-start | bytes 262144 | tf_op jit(solution)/shard_map/psum | solution.py:84
  9.2 17.4 %collective-permute-start = (bf16[1,1024,128]{2,1,0:T(8,128)(2,1)S(1)}, bf16[1,1024,128]{2,1,0:T(8,128)(2,1)S(1)}, u32[]{:S(2)}, u32[]{:S(2)}) collective-permute-start(bf16[1,1024,128]{2,1,0:T(8,128)(2,1)S(1)} %bitcast.271), channel_id=1, source_target_pairs={{0,2},{2,4},{4,6},{6,8},{8,10},{10,12},{12,14},{14,16},{16,18},{18... | collective-permute-start | bytes 786440 | tf_op jit(solution)/shard_map/ppermute | solution.py:17
  11.6 15.7 %collective-permute-start.1 = (bf16[1,1024,128]{2,1,0:T(8,128)(2,1)S(1)}, bf16[1,1024,128]{2,1,0:T(8,128)(2,1)S(1)}, u32[]{:S(2)}, u32[]{:S(2)}) collective-permute-start(bf16[1,1024,128]{2,1,0:T(8,128)(2,1)S(1)} %bitcast.272), channel_id=1, source_target_pairs={{2,0},{4,2},{6,4},{8,6},{10,8},{12,10},{14,12},{16,14},{18,16},{20... | collective-permute-start | bytes 786440 | tf_op jit(solution)/shard_map/ppermute | solution.py:19
  32.7 5.2 %copy-start.5 = (f32[1024]{0:T(1024)S(1)}, f32[1024]{0:T(1024)}, u32[]{:S(2)}) copy-start(f32[1024]{0:T(1024)} %param.9) | copy-start | bytes 12292
  35.9 2.1 copy-start.1
  40.0 13.0 %collective-permute-start.2 = (bf16[1,1024,128]{2,1,0:T(8,128)(2,1)S(1)}, bf16[1,1024,128]{2,1,0:T(8,128)(2,1)}, u32[]{:S(2)}, u32[]{:S(2)}) collective-permute-start(bf16[1,1024,128]{2,1,0:T(8,128)(2,1)S(1)} %bitcast.273), channel_id=1, source_target_pairs={{0,2},{2,4},{4,6},{6,8},{8,10},{10,12},{12,14},{14,16},{16,18},{18... | collective-permute-start | bytes 786440 | tf_op jit(solution)/shard_map/ppermute | solution.py:17
  44.4 10.3 %collective-permute-start.3 = (bf16[1,1024,128]{2,1,0:T(8,128)(2,1)S(1)}, bf16[1,1024,128]{2,1,0:T(8,128)(2,1)}, u32[]{:S(2)}, u32[]{:S(2)}) collective-permute-start(bf16[1,1024,128]{2,1,0:T(8,128)(2,1)S(1)} %bitcast.274), channel_id=1, source_target_pairs={{2,0},{4,2},{6,4},{8,6},{10,8},{12,10},{14,12},{16,14},{18,16},{20... | collective-permute-start | bytes 786440 | tf_op jit(solution)/shard_map/ppermute | solution.py:19
  68.7 13.5 %collective-permute-start.4 = (bf16[1,1024,128]{2,1,0:T(8,128)(2,1)S(1)}, bf16[1,1024,128]{2,1,0:T(8,128)(2,1)}, u32[]{:S(2)}, u32[]{:S(2)}) collective-permute-start(bf16[1,1024,128]{2,1,0:T(8,128)(2,1)S(1)} %bitcast.269), channel_id=1, source_target_pairs={{0,2},{2,4},{4,6},{6,8},{8,10},{10,12},{12,14},{14,16},{16,18},{18... | collective-permute-start | bytes 786440 | tf_op jit(solution)/shard_map/ppermute | solution.py:17
  73.8 10.1 %collective-permute-start.5 = (bf16[1,1024,128]{2,1,0:T(8,128)(2,1)S(1)}, bf16[1,1024,128]{2,1,0:T(8,128)(2,1)}, u32[]{:S(2)}, u32[]{:S(2)}) collective-permute-start(bf16[1,1024,128]{2,1,0:T(8,128)(2,1)S(1)} %bitcast.270), channel_id=1, source_target_pairs={{2,0},{4,2},{6,4},{8,6},{10,8},{12,10},{14,12},{16,14},{18,16},{20... | collective-permute-start | bytes 786440 | tf_op jit(solution)/shard_map/ppermute | solution.py:19
  98.1 13.6 %collective-permute-start.6 = (bf16[1,1024,128]{2,1,0:T(8,128)(2,1)S(1)}, bf16[1,1024,128]{2,1,0:T(8,128)(2,1)S(1)}, u32[]{:S(2)}, u32[]{:S(2)}) collective-permute-start(bf16[1,1024,128]{2,1,0:T(8,128)(2,1)S(1)} %bitcast.275), channel_id=1, source_target_pairs={{0,2},{2,4},{4,6},{6,8},{8,10},{10,12},{12,14},{14,16},{16,18},{18... | collective-permute-start | bytes 786440 | tf_op jit(solution)/shard_map/ppermute | solution.py:17
  103.3 9.2 %collective-permute-start.7 = (bf16[1,1024,128]{2,1,0:T(8,128)(2,1)S(1)}, bf16[1,1024,128]{2,1,0:T(8,128)(2,1)S(1)}, u32[]{:S(2)}, u32[]{:S(2)}) collective-permute-start(bf16[1,1024,128]{2,1,0:T(8,128)(2,1)S(1)} %bitcast.276), channel_id=1, source_target_pairs={{2,0},{4,2},{6,4},{8,6},{10,8},{12,10},{14,12},{16,14},{18,16},{20... | collective-permute-start | bytes 786440 | tf_op jit(solution)/shard_map/ppermute | solution.py:19
  121.1 2.1 copy-start.3
  125.6 14.4 %collective-permute-start.8 = (bf16[1,1024,128]{2,1,0:T(8,128)(2,1)S(1)}, bf16[1,1024,128]{2,1,0:T(8,128)(2,1)S(1)}, u32[]{:S(2)}, u32[]{:S(2)}) collective-permute-start(bf16[1,1024,128]{2,1,0:T(8,128)(2,1)S(1)} %bitcast.277), channel_id=1, source_target_pairs={{0,2},{2,4},{4,6},{6,8},{8,10},{10,12},{12,14},{14,16},{16,18},{18... | collective-permute-start | bytes 786440 | tf_op jit(solution)/shard_map/ppermute | solution.py:17
  131.6 9.2 %collective-permute-start.9 = (bf16[1,1024,128]{2,1,0:T(8,128)(2,1)S(1)}, bf16[1,1024,128]{2,1,0:T(8,128)(2,1)S(1)}, u32[]{:S(2)}, u32[]{:S(2)}) collective-permute-start(bf16[1,1024,128]{2,1,0:T(8,128)(2,1)S(1)} %bitcast.278), channel_id=1, source_target_pairs={{2,0},{4,2},{6,4},{8,6},{10,8},{12,10},{14,12},{16,14},{18,16},{20... | collective-permute-start | bytes 786440 | tf_op jit(solution)/shard_map/ppermute | solution.py:19
  151.9 58.7 %copy-start.2 = (f32[1024,128]{1,0:T(8,128)}, f32[1024,128]{1,0:T(8,128)S(1)}, u32[]{:S(2)}) copy-start(f32[1024,128]{1,0:T(8,128)S(1)} %get-tuple-element.27) | copy-start | bytes 1572868
  151.9 15.2 %collective-permute-start.10 = (bf16[1,1024,128]{2,1,0:T(8,128)(2,1)S(1)}, bf16[1,1024,128]{2,1,0:T(8,128)(2,1)}, u32[]{:S(2)}, u32[]{:S(2)}) collective-permute-start(bf16[1,1024,128]{2,1,0:T(8,128)(2,1)S(1)} %bitcast.279), channel_id=1, source_target_pairs={{0,2},{2,4},{4,6},{6,8},{8,10},{10,12},{12,14},{14,16},{16,18},{18... | collective-permute-start | bytes 786440 | tf_op jit(solution)/shard_map/ppermute | solution.py:17
  158.7 10.1 %collective-permute-start.11 = (bf16[1,1024,128]{2,1,0:T(8,128)(2,1)S(1)}, bf16[1,1024,128]{2,1,0:T(8,128)(2,1)}, u32[]{:S(2)}, u32[]{:S(2)}) collective-permute-start(bf16[1,1024,128]{2,1,0:T(8,128)(2,1)S(1)} %bitcast.280), channel_id=1, source_target_pairs={{2,0},{4,2},{6,4},{8,6},{10,8},{12,10},{14,12},{16,14},{18,16},{20... | collective-permute-start | bytes 786440 | tf_op jit(solution)/shard_map/ppermute | solution.py:19
  182.8 14.6 %collective-permute-start.12 = (bf16[1,1024,128]{2,1,0:T(8,128)(2,1)S(1)}, bf16[1,1024,128]{2,1,0:T(8,128)(2,1)}, u32[]{:S(2)}, u32[]{:S(2)}) collective-permute-start(bf16[1,1024,128]{2,1,0:T(8,128)(2,1)S(1)} %bitcast.281), channel_id=1, source_target_pairs={{0,2},{2,4},{4,6},{6,8},{8,10},{10,12},{12,14},{14,16},{16,18},{18... | collective-permute-start | bytes 786440 | tf_op jit(solution)/shard_map/ppermute | solution.py:17
  188.8 10.3 %collective-permute-start.13 = (bf16[1,1024,128]{2,1,0:T(8,128)(2,1)S(1)}, bf16[1,1024,128]{2,1,0:T(8,128)(2,1)}, u32[]{:S(2)}, u32[]{:S(2)}) collective-permute-start(bf16[1,1024,128]{2,1,0:T(8,128)(2,1)S(1)} %bitcast.282), channel_id=1, source_target_pairs={{2,0},{4,2},{6,4},{8,6},{10,8},{12,10},{14,12},{16,14},{18,16},{20... | collective-permute-start | bytes 786440 | tf_op jit(solution)/shard_map/ppermute | solution.py:19
  212.9 13.7 %collective-permute-start.14 = (bf16[1,1024,128]{2,1,0:T(8,128)(2,1)S(1)}, bf16[1,1024,128]{2,1,0:T(8,128)(2,1)S(1)}, u32[]{:S(2)}, u32[]{:S(2)}) collective-permute-start(bf16[1,1024,128]{2,1,0:T(8,128)(2,1)S(1)} %bitcast.267), channel_id=1, source_target_pairs={{0,2},{2,4},{4,6},{6,8},{8,10},{10,12},{12,14},{14,16},{16,18},{18... | collective-permute-start | bytes 786440 | tf_op jit(solution)/shard_map/ppermute | solution.py:17
  218.2 9.2 %collective-permute-start.15 = (bf16[1,1024,128]{2,1,0:T(8,128)(2,1)S(1)}, bf16[1,1024,128]{2,1,0:T(8,128)(2,1)S(1)}, u32[]{:S(2)}, u32[]{:S(2)}) collective-permute-start(bf16[1,1024,128]{2,1,0:T(8,128)(2,1)S(1)} %bitcast.268), channel_id=1, source_target_pairs={{2,0},{4,2},{6,4},{8,6},{10,8},{12,10},{14,12},{16,14},{18,16},{20... | collective-permute-start | bytes 786440 | tf_op jit(solution)/shard_map/ppermute | solution.py:19
  238.0 15.3 %collective-permute-start.16 = (bf16[1,1024,128]{2,1,0:T(8,128)(2,1)S(1)}, bf16[1,1024,128]{2,1,0:T(8,128)(2,1)S(1)}, u32[]{:S(2)}, u32[]{:S(2)}) collective-permute-start(bf16[1,1024,128]{2,1,0:T(8,128)(2,1)S(1)} %bitcast.265), channel_id=1, source_target_pairs={{0,2},{2,4},{4,6},{6,8},{8,10},{10,12},{12,14},{14,16},{16,18},{18... | collective-permute-start | bytes 786440 | tf_op jit(solution)/shard_map/ppermute | solution.py:17
  243.2 10.2 %collective-permute-start.17 = (bf16[1,1024,128]{2,1,0:T(8,128)(2,1)S(1)}, bf16[1,1024,128]{2,1,0:T(8,128)(2,1)S(1)}, u32[]{:S(2)}, u32[]{:S(2)}) collective-permute-start(bf16[1,1024,128]{2,1,0:T(8,128)(2,1)S(1)} %bitcast.266), channel_id=1, source_target_pairs={{2,0},{4,2},{6,4},{8,6},{10,8},{12,10},{14,12},{16,14},{18,16},{20... | collective-permute-start | bytes 786440 | tf_op jit(solution)/shard_map/ppermute | solution.py:19
  253.6 1.1 copy-start.4
  395.0 26.3 %copy-start.6 = (f32[128,128]{1,0:T(8,128)S(1)}, f32[128,128]{1,0:T(8,128)}, u32[]{:S(2)}) copy-start(f32[128,128]{1,0:T(8,128)} %get-tuple-element.3) | copy-start | bytes 196612
Sparse Core Ops, SparseCore 0:
  266.0 128.9 all-reduce.2
where the time goes:
time: 432 us; the launch traced here: 429 us
  waiting for transfers between devices  129 us (30%)
  local copies, waits for them, and re-layouts  67.9 us (16%)
  blocking collectives  64.9 us (15%)
  other arithmetic  59.2 us (14%)
  starting transfers between devices  57.9 us (13%)
  matrix products  32.6 us (8%)
  between operations  17.6 us (4%)
    psum x1, waiting for transfers between devices, per_device(): gram = lax.psum(gram_local, ('row', 'col'))  129 us
    all_gather x9, blocking collectives, coupled(): line = lax.all_gather(rounded[None], 'col', axis=0, tiled=True)  64.9 us
    ppermute x9, starting transfers between devices, with_halo(): lax.ppermute(tail, axis, [(i, (i + 1) % count) for i in range(ends)])  46.3 us
    gather x9, local copies, waits for them, and re-layouts, coupled(): picked = stack[tile_cols]  28.6 us
    unnamed x18, other arithmetic  26.7 us
    dot_general x9, matrix products, coupled(): jnp.einsum('psab,psbk->pak', couplings, picked, preferred_element_type=jn...  26.4 us
    unnamed x32, local copies, waits for them, and re-layouts  20.4 us
    dot_general x9, local copies, waits for them, and re-layouts, coupled(): jnp.einsum('psab,psbk->pak', couplings, picked, preferred_element_type=jn...  16.6 us
  transfers between devices with their start and end apart: 19, of which 1 were waited for; matrix products, arithmetic and copies ran while one was open for 3% of the time, Pallas kernels for 0%

commit v1 on v0

--- a/solution.py
+++ b/solution.py
@@ -81,7 +81,8 @@
     weighted = masses[:, None] / node_count
     identity = jnp.eye(vec_width, dtype=jnp.float32)
     gram_local = matmul_high(current.T, weighted * current)
-    gram = lax.psum(gram_local, ("row", "col"))
+    half = lax.psum(gram_local, "col")
+    gram = lax.psum(half, "row")
     projected = lax.psum(matmul_high(current.T, stiff(current) / node_count), ("row", "col"))
     inverse = cholesky_inverse(gram, identity)
     basis = matmul_high(current, inverse.T)

time: 432 us -> 532 us (1.23)
  waiting for transfers between devices: 129 us -> 218 us
    psum x1 -> x3, waiting for transfers between devices: 129 us -> 218 us  [the longest x1 119 us: per_device(): lax.psum(matmul_high(current.T, stiff(current) / node_count), ('row', 'co...]
    unnamed x32 -> x30, local copies, waits for them, and re-layouts: 20.4 us -> 22.6 us
  transfers between devices with their start and end apart: 19 -> 21, of which waited for: 1 -> 3; matrix products, arithmetic and copies ran while one was open for 3% -> 8% of each run, Pallas kernels for 0% -> 0%
where the time goes in v1:
time: 532 us; the launch traced here: 528 us
  waiting for transfers between devices  218 us (41%)
  local copies, waits for them, and re-layouts  69.9 us (13%)
  blocking collectives  66.2 us (12%)
  other arithmetic  61.8 us (12%)
  starting transfers between devices  58.7 us (11%)
  matrix products  34.3 us (6%)
  between operations  19.1 us (4%)
    psum x1, waiting for transfers between devices, per_device(): lax.psum(matmul_high(current.T, stiff(current) / node_count), ('row', 'co...  119 us
    psum x1, waiting for transfers between devices, per_device(): gram = lax.psum(half, 'row')  81.3 us
    all_gather x9, blocking collectives, coupled(): line = lax.all_gather(rounded[None], 'col', axis=0, tiled=True)  66.2 us
    ppermute x9, starting transfers between devices, with_halo(): lax.ppermute(tail, axis, [(i, (i + 1) % count) for i in range(ends)])  47 us
    gather x9, local copies, waits for them, and re-layouts, coupled(): picked = stack[tile_cols]  28.6 us
    unnamed x18, other arithmetic  28.1 us
    dot_general x9, matrix products, coupled(): jnp.einsum('psab,psbk->pak', couplings, picked, preferred_element_type=jn...  26.4 us
    unnamed x30, local copies, waits for them, and re-layouts  22.6 us
  transfers between devices with their start and end apart: 21, of which 3 were waited for; matrix products, arithmetic and copies ran while one was open for 8% of the time, Pallas kernels for 0%

profile of v1, /device:TPU:0, one launch (start us, length us, event | category | flops | bytes accessed | tf_op | source)
XLA Modules:
  0.0 528.1 jit_solution(516226413662762454)
XLA Ops:
  19.2 8.2 %all-gather = bf16[2048,128]{1,0:T(8,128)(2,1)S(1)} all-gather(bf16[1024,128]{1,0:T(8,128)(2,1)S(1)} %get-tuple-element.15), channel_id=2, replica_groups=mesh['row'=16,'col'=2] {'col'}, dimensions={0}, use_global_device_ids=true | all-gather | bytes 786432 | tf_op jit(solution)/shard_map/all_gather | solution.py:43
  30.4 3.2 gather_fusion
  40.9 4.3 collective-permute-start.2
  46.7 7.2 %all-gather.1 = bf16[2048,128]{1,0:T(8,128)(2,1)S(1)} all-gather(bf16[1024,128]{1,0:T(8,128)(2,1)S(1)} %get-tuple-element.21), channel_id=3, replica_groups=mesh['row'=16,'col'=2] {'col'}, dimensions={0}, use_global_device_ids=true | all-gather | bytes 786432 | tf_op jit(solution)/shard_map/all_gather | solution.py:43
  58.7 3.2 gather_fusion.1
  69.5 5.1 collective-permute-start.4
  76.0 7.0 %all-gather.2 = bf16[2048,128]{1,0:T(8,128)(2,1)S(1)} all-gather(bf16[1024,128]{1,0:T(8,128)(2,1)S(1)} %get-tuple-element.13), channel_id=4, replica_groups=mesh['row'=16,'col'=2] {'col'}, dimensions={0}, use_global_device_ids=true | all-gather | bytes 786432 | tf_op jit(solution)/shard_map/all_gather | solution.py:43
  87.9 3.2 gather_fusion.2
  98.8 5.2 collective-permute-start.6
  105.5 7.0 %all-gather.3 = bf16[2048,128]{1,0:T(8,128)(2,1)S(1)} all-gather(bf16[1024,128]{1,0:T(8,128)(2,1)S(1)} %get-tuple-element.11), channel_id=5, replica_groups=mesh['row'=16,'col'=2] {'col'}, dimensions={0}, use_global_device_ids=true | all-gather | bytes 786432 | tf_op jit(solution)/shard_map/all_gather | solution.py:43
  115.5 3.2 gather_fusion.3
  126.3 6.0 %collective-permute-start.8 = (bf16[1,1024,128]{2,1,0:T(8,128)(2,1)S(1)}, bf16[1,1024,128]{2,1,0:T(8,128)(2,1)S(1)}, u32[]{:S(2)}, u32[]{:S(2)}) collective-permute-start(bf16[1,1024,128]{2,1,0:T(8,128)(2,1)S(1)} %bitcast.277), channel_id=1, source_target_pairs={{0,2},{2,4},{4,6},{6,8},{8,10},{10,12},{12,14},{14,16},{16,18},{18... | collective-permute-start | bytes 786440 | tf_op jit(solution)/shard_map/ppermute | solution.py:17
  133.7 7.0 %all-gather.4 = bf16[2048,128]{1,0:T(8,128)(2,1)S(1)} all-gather(bf16[1024,128]{1,0:T(8,128)(2,1)S(1)} %get-tuple-element.9), channel_id=6, replica_groups=mesh['row'=16,'col'=2] {'col'}, dimensions={0}, use_global_device_ids=true | all-gather | bytes 786432 | tf_op jit(solution)/shard_map/all_gather | solution.py:43
  143.7 3.2 gather_fusion.4
  152.6 6.7 %collective-permute-start.10 = (bf16[1,1024,128]{2,1,0:T(8,128)(2,1)S(1)}, bf16[1,1024,128]{2,1,0:T(8,128)(2,1)}, u32[]{:S(2)}, u32[]{:S(2)}) collective-permute-start(bf16[1,1024,128]{2,1,0:T(8,128)(2,1)S(1)} %bitcast.279), channel_id=1, source_target_pairs={{0,2},{2,4},{4,6},{6,8},{8,10},{10,12},{12,14},{14,16},{16,18},{18... | collective-permute-start | bytes 786440 | tf_op jit(solution)/shard_map/ppermute | solution.py:17
  160.7 7.0 %all-gather.5 = bf16[2048,128]{1,0:T(8,128)(2,1)S(1)} all-gather(bf16[1024,128]{1,0:T(8,128)(2,1)S(1)} %get-tuple-element.7), channel_id=7, replica_groups=mesh['row'=16,'col'=2] {'col'}, dimensions={0}, use_global_device_ids=true | all-gather | bytes 786432 | tf_op jit(solution)/shard_map/all_gather | solution.py:43
  172.6 3.2 gather_fusion.5
  175.8 3.1 convolution_bitcast_fusion.3
  183.4 6.0 %collective-permute-start.12 = (bf16[1,1024,128]{2,1,0:T(8,128)(2,1)S(1)}, bf16[1,1024,128]{2,1,0:T(8,128)(2,1)}, u32[]{:S(2)}, u32[]{:S(2)}) collective-permute-start(bf16[1,1024,128]{2,1,0:T(8,128)(2,1)S(1)} %bitcast.281), channel_id=1, source_target_pairs={{0,2},{2,4},{4,6},{6,8},{8,10},{10,12},{12,14},{14,16},{16,18},{18... | collective-permute-start | bytes 786440 | tf_op jit(solution)/shard_map/ppermute | solution.py:17
  190.8 7.2 %all-gather.6 = bf16[2048,128]{1,0:T(8,128)(2,1)S(1)} all-gather(bf16[1024,128]{1,0:T(8,128)(2,1)S(1)} %get-tuple-element.5), channel_id=8, replica_groups=mesh['row'=16,'col'=2] {'col'}, dimensions={0}, use_global_device_ids=true | all-gather | bytes 786432 | tf_op jit(solution)/shard_map/all_gather | solution.py:43
  202.9 3.2 gather_fusion.6
  213.5 5.3 %collective-permute-start.14 = (bf16[1,1024,128]{2,1,0:T(8,128)(2,1)S(1)}, bf16[1,1024,128]{2,1,0:T(8,128)(2,1)S(1)}, u32[]{:S(2)}, u32[]{:S(2)}) collective-permute-start(bf16[1,1024,128]{2,1,0:T(8,128)(2,1)S(1)} %bitcast.267), channel_id=1, source_target_pairs={{0,2},{2,4},{4,6},{6,8},{8,10},{10,12},{12,14},{14,16},{16,18},{18... | collective-permute-start | bytes 786440 | tf_op jit(solution)/shard_map/ppermute | solution.py:17
  220.2 7.0 %all-gather.7 = bf16[2048,128]{1,0:T(8,128)(2,1)S(1)} all-gather(bf16[1024,128]{1,0:T(8,128)(2,1)S(1)} %get-tuple-element.28), channel_id=9, replica_groups=mesh['row'=16,'col'=2] {'col'}, dimensions={0}, use_global_device_ids=true | all-gather | bytes 786432 | tf_op jit(solution)/shard_map/all_gather | solution.py:43
  230.2 3.2 gather_fusion.7
  241.2 5.9 %collective-permute-start.16 = (bf16[1,1024,128]{2,1,0:T(8,128)(2,1)S(1)}, bf16[1,1024,128]{2,1,0:T(8,128)(2,1)}, u32[]{:S(2)}, u32[]{:S(2)}) collective-permute-start(bf16[1,1024,128]{2,1,0:T(8,128)(2,1)S(1)} %bitcast.265), channel_id=1, source_target_pairs={{0,2},{2,4},{4,6},{6,8},{8,10},{10,12},{12,14},{14,16},{16,18},{18... | collective-permute-start | bytes 786440 | tf_op jit(solution)/shard_map/ppermute | solution.py:17
  248.3 17.6 %all-reduce.4.cloned.1.call-done = f32[128,128]{0,1:T(8,128)} async-done(((f32[128,128]{0,1:T(8,128)}), f32[128,128]{0,1:T(8,128)}) %all-reduce.4.cloned.1.call-update) | async-done | bytes 65552 | tf_op jit(solution)/shard_map/psum | solution.py:84
  266.0 8.4 %all-gather.8 = bf16[2048,128]{1,0:T(8,128)(2,1)} all-gather(bf16[1024,128]{1,0:T(8,128)(2,1)S(1)} %get-tuple-element.3), channel_id=10, replica_groups=mesh['row'=16,'col'=2] {'col'}, dimensions={0}, use_global_device_ids=true | all-gather | bytes 786432 | tf_op jit(solution)/shard_map/all_gather | solution.py:43
  274.4 81.3 %all-reduce.6.cloned.1.call-done = f32[128,128]{0,1:T(8,128)} async-done(((f32[128,128]{0,1:T(8,128)}), f32[128,128]{0,1:T(8,128)}) %all-reduce.6.cloned.1.call-update) | async-done | bytes 65552 | tf_op jit(solution)/shard_map/psum | solution.py:85
  357.4 11.7 %cholesky.17 = f32[128,128]{1,0:T(8,128)S(1)} custom-call(f32[128,128]{1,0:T(8,128)S(1)} %fusion.38), custom_call_target="Cholesky" | custom-call | tf_op jit(solution)/shard_map/jit(cholesky)/cholesky | solution.py:31
  370.5 10.4 %custom-call.6 = f32[1,128,128]{1,2,0:T(8,128)} custom-call(f32[1,128,128]{2,1,0:T(8,128)S(1)} %fusion.35), custom_call_target="InvertDiagBlocksLowerTriangular" | custom-call | tf_op jit(solution)/shard_map/triangular_solve | solution.py:32
  387.0 3.2 gather_fusion.8
  399.6 119.1 %all-reduce.8.cloned.1.call-done = f32[128,128]{1,0:T(8,128)} async-done(((f32[128,128]{1,0:T(8,128)}), f32[128,128]{1,0:T(8,128)}) %all-reduce.8.cloned.1.call-update) | async-done | bytes 65552 | tf_op jit(solution)/shard_map/psum | solution.py:86
  (125 shorter events, 126.4 us)
Async XLA Ops:
  8.0 25.6 %copy-start = (bf16[4,5,256,256]{3,2,1,0:T(8,128)(2,1)S(1)}, bf16[4,5,256,256]{3,2,1,0:T(8,128)(2,1)}, u32[]{:S(2)}) copy-start(bf16[4,5,256,256]{3,2,1,0:T(8,128)(2,1)} %param.7) | copy-start | bytes 7864324
  8.0 258.0 %all-reduce.4.cloned.1.call-start = ((), (), s32[]{:S(2)}) async-start(), calls=%async_computation | async-start | bytes 131072 | tf_op jit(solution)/shard_map/psum | solution.py:84
  10.0 17.4 %collective-permute-start = (bf16[1,1024,128]{2,1,0:T(8,128)(2,1)S(1)}, bf16[1,1024,128]{2,1,0:T(8,128)(2,1)S(1)}, u32[]{:S(2)}, u32[]{:S(2)}) collective-permute-start(bf16[1,1024,128]{2,1,0:T(8,128)(2,1)S(1)} %bitcast.271), channel_id=1, source_target_pairs={{0,2},{2,4},{4,6},{6,8},{8,10},{10,12},{12,14},{14,16},{16,18},{18... | collective-permute-start | bytes 786440 | tf_op jit(solution)/shard_map/ppermute | solution.py:17
  12.4 15.7 %collective-permute-start.1 = (bf16[1,1024,128]{2,1,0:T(8,128)(2,1)S(1)}, bf16[1,1024,128]{2,1,0:T(8,128)(2,1)S(1)}, u32[]{:S(2)}, u32[]{:S(2)}) collective-permute-start(bf16[1,1024,128]{2,1,0:T(8,128)(2,1)S(1)} %bitcast.272), channel_id=1, source_target_pairs={{2,0},{4,2},{6,4},{8,6},{10,8},{12,10},{14,12},{16,14},{18,16},{20... | collective-permute-start | bytes 786440 | tf_op jit(solution)/shard_map/ppermute | solution.py:19
  33.5 5.2 copy-start.5
  36.7 2.1 copy-start.1
  40.9 13.0 %collective-permute-start.2 = (bf16[1,1024,128]{2,1,0:T(8,128)(2,1)S(1)}, bf16[1,1024,128]{2,1,0:T(8,128)(2,1)}, u32[]{:S(2)}, u32[]{:S(2)}) collective-permute-start(bf16[1,1024,128]{2,1,0:T(8,128)(2,1)S(1)} %bitcast.273), channel_id=1, source_target_pairs={{0,2},{2,4},{4,6},{6,8},{8,10},{10,12},{12,14},{14,16},{16,18},{18... | collective-permute-start | bytes 786440 | tf_op jit(solution)/shard_map/ppermute | solution.py:17
  45.2 10.3 %collective-permute-start.3 = (bf16[1,1024,128]{2,1,0:T(8,128)(2,1)S(1)}, bf16[1,1024,128]{2,1,0:T(8,128)(2,1)}, u32[]{:S(2)}, u32[]{:S(2)}) collective-permute-start(bf16[1,1024,128]{2,1,0:T(8,128)(2,1)S(1)} %bitcast.274), channel_id=1, source_target_pairs={{2,0},{4,2},{6,4},{8,6},{10,8},{12,10},{14,12},{16,14},{18,16},{20... | collective-permute-start | bytes 786440 | tf_op jit(solution)/shard_map/ppermute | solution.py:19
  69.5 13.5 %collective-permute-start.4 = (bf16[1,1024,128]{2,1,0:T(8,128)(2,1)S(1)}, bf16[1,1024,128]{2,1,0:T(8,128)(2,1)}, u32[]{:S(2)}, u32[]{:S(2)}) collective-permute-start(bf16[1,1024,128]{2,1,0:T(8,128)(2,1)S(1)} %bitcast.269), channel_id=1, source_target_pairs={{0,2},{2,4},{4,6},{6,8},{8,10},{10,12},{12,14},{14,16},{16,18},{18... | collective-permute-start | bytes 786440 | tf_op jit(solution)/shard_map/ppermute | solution.py:17
  74.6 10.1 %collective-permute-start.5 = (bf16[1,1024,128]{2,1,0:T(8,128)(2,1)S(1)}, bf16[1,1024,128]{2,1,0:T(8,128)(2,1)}, u32[]{:S(2)}, u32[]{:S(2)}) collective-permute-start(bf16[1,1024,128]{2,1,0:T(8,128)(2,1)S(1)} %bitcast.270), channel_id=1, source_target_pairs={{2,0},{4,2},{6,4},{8,6},{10,8},{12,10},{14,12},{16,14},{18,16},{20... | collective-permute-start | bytes 786440 | tf_op jit(solution)/shard_map/ppermute | solution.py:19
  98.8 13.7 %collective-permute-start.6 = (bf16[1,1024,128]{2,1,0:T(8,128)(2,1)S(1)}, bf16[1,1024,128]{2,1,0:T(8,128)(2,1)S(1)}, u32[]{:S(2)}, u32[]{:S(2)}) collective-permute-start(bf16[1,1024,128]{2,1,0:T(8,128)(2,1)S(1)} %bitcast.275), channel_id=1, source_target_pairs={{0,2},{2,4},{4,6},{6,8},{8,10},{10,12},{12,14},{14,16},{16,18},{18... | collective-permute-start | bytes 786440 | tf_op jit(solution)/shard_map/ppermute | solution.py:17
  104.1 9.2 %collective-permute-start.7 = (bf16[1,1024,128]{2,1,0:T(8,128)(2,1)S(1)}, bf16[1,1024,128]{2,1,0:T(8,128)(2,1)S(1)}, u32[]{:S(2)}, u32[]{:S(2)}) collective-permute-start(bf16[1,1024,128]{2,1,0:T(8,128)(2,1)S(1)} %bitcast.276), channel_id=1, source_target_pairs={{2,0},{4,2},{6,4},{8,6},{10,8},{12,10},{14,12},{16,14},{18,16},{20... | collective-permute-start | bytes 786440 | tf_op jit(solution)/shard_map/ppermute | solution.py:19
  121.8 2.1 copy-start.3
  126.3 14.4 %collective-permute-start.8 = (bf16[1,1024,128]{2,1,0:T(8,128)(2,1)S(1)}, bf16[1,1024,128]{2,1,0:T(8,128)(2,1)S(1)}, u32[]{:S(2)}, u32[]{:S(2)}) collective-permute-start(bf16[1,1024,128]{2,1,0:T(8,128)(2,1)S(1)} %bitcast.277), channel_id=1, source_target_pairs={{0,2},{2,4},{4,6},{6,8},{8,10},{10,12},{12,14},{14,16},{16,18},{18... | collective-permute-start | bytes 786440 | tf_op jit(solution)/shard_map/ppermute | solution.py:17
  132.3 9.2 %collective-permute-start.9 = (bf16[1,1024,128]{2,1,0:T(8,128)(2,1)S(1)}, bf16[1,1024,128]{2,1,0:T(8,128)(2,1)S(1)}, u32[]{:S(2)}, u32[]{:S(2)}) collective-permute-start(bf16[1,1024,128]{2,1,0:T(8,128)(2,1)S(1)} %bitcast.278), channel_id=1, source_target_pairs={{2,0},{4,2},{6,4},{8,6},{10,8},{12,10},{14,12},{16,14},{18,16},{20... | collective-permute-start | bytes 786440 | tf_op jit(solution)/shard_map/ppermute | solution.py:19
  152.6 58.6 %copy-start.2 = (f32[1024,128]{1,0:T(8,128)}, f32[1024,128]{1,0:T(8,128)S(1)}, u32[]{:S(2)}) copy-start(f32[1024,128]{1,0:T(8,128)S(1)} %get-tuple-element.25) | copy-start | bytes 1572868
  152.6 15.1 %collective-permute-start.10 = (bf16[1,1024,128]{2,1,0:T(8,128)(2,1)S(1)}, bf16[1,1024,128]{2,1,0:T(8,128)(2,1)}, u32[]{:S(2)}, u32[]{:S(2)}) collective-permute-start(bf16[1,1024,128]{2,1,0:T(8,128)(2,1)S(1)} %bitcast.279), channel_id=1, source_target_pairs={{0,2},{2,4},{4,6},{6,8},{8,10},{10,12},{12,14},{14,16},{16,18},{18... | collective-permute-start | bytes 786440 | tf_op jit(solution)/shard_map/ppermute | solution.py:17
  159.3 10.1 %collective-permute-start.11 = (bf16[1,1024,128]{2,1,0:T(8,128)(2,1)S(1)}, bf16[1,1024,128]{2,1,0:T(8,128)(2,1)}, u32[]{:S(2)}, u32[]{:S(2)}) collective-permute-start(bf16[1,1024,128]{2,1,0:T(8,128)(2,1)S(1)} %bitcast.280), channel_id=1, source_target_pairs={{2,0},{4,2},{6,4},{8,6},{10,8},{12,10},{14,12},{16,14},{18,16},{20... | collective-permute-start | bytes 786440 | tf_op jit(solution)/shard_map/ppermute | solution.py:19
  183.4 14.6 %collective-permute-start.12 = (bf16[1,1024,128]{2,1,0:T(8,128)(2,1)S(1)}, bf16[1,1024,128]{2,1,0:T(8,128)(2,1)}, u32[]{:S(2)}, u32[]{:S(2)}) collective-permute-start(bf16[1,1024,128]{2,1,0:T(8,128)(2,1)S(1)} %bitcast.281), channel_id=1, source_target_pairs={{0,2},{2,4},{4,6},{6,8},{8,10},{10,12},{12,14},{14,16},{16,18},{18... | collective-permute-start | bytes 786440 | tf_op jit(solution)/shard_map/ppermute | solution.py:17
  189.4 10.3 %collective-permute-start.13 = (bf16[1,1024,128]{2,1,0:T(8,128)(2,1)S(1)}, bf16[1,1024,128]{2,1,0:T(8,128)(2,1)}, u32[]{:S(2)}, u32[]{:S(2)}) collective-permute-start(bf16[1,1024,128]{2,1,0:T(8,128)(2,1)S(1)} %bitcast.282), channel_id=1, source_target_pairs={{2,0},{4,2},{6,4},{8,6},{10,8},{12,10},{14,12},{16,14},{18,16},{20... | collective-permute-start | bytes 786440 | tf_op jit(solution)/shard_map/ppermute | solution.py:19
  213.5 13.7 %collective-permute-start.14 = (bf16[1,1024,128]{2,1,0:T(8,128)(2,1)S(1)}, bf16[1,1024,128]{2,1,0:T(8,128)(2,1)S(1)}, u32[]{:S(2)}, u32[]{:S(2)}) collective-permute-start(bf16[1,1024,128]{2,1,0:T(8,128)(2,1)S(1)} %bitcast.267), channel_id=1, source_target_pairs={{0,2},{2,4},{4,6},{6,8},{8,10},{10,12},{12,14},{14,16},{16,18},{18... | collective-permute-start | bytes 786440 | tf_op jit(solution)/shard_map/ppermute | solution.py:17
  218.8 9.2 %collective-permute-start.15 = (bf16[1,1024,128]{2,1,0:T(8,128)(2,1)S(1)}, bf16[1,1024,128]{2,1,0:T(8,128)(2,1)S(1)}, u32[]{:S(2)}, u32[]{:S(2)}) collective-permute-start(bf16[1,1024,128]{2,1,0:T(8,128)(2,1)S(1)} %bitcast.268), channel_id=1, source_target_pairs={{2,0},{4,2},{6,4},{8,6},{10,8},{12,10},{14,12},{16,14},{18,16},{20... | collective-permute-start | bytes 786440 | tf_op jit(solution)/shard_map/ppermute | solution.py:19
  241.1 114.5 %all-reduce.6.cloned.1.call-start = ((), (), s32[]{:S(2)}) async-start(), calls=%async_computation.1 | async-start | bytes 131072 | tf_op jit(solution)/shard_map/psum | solution.py:85
  241.2 140.9 %collective-permute-start.16 = (bf16[1,1024,128]{2,1,0:T(8,128)(2,1)S(1)}, bf16[1,1024,128]{2,1,0:T(8,128)(2,1)}, u32[]{:S(2)}, u32[]{:S(2)}) collective-permute-start(bf16[1,1024,128]{2,1,0:T(8,128)(2,1)S(1)} %bitcast.265), channel_id=1, source_target_pairs={{0,2},{2,4},{4,6},{6,8},{8,10},{10,12},{12,14},{14,16},{16,18},{18... | collective-permute-start | bytes 786440 | tf_op jit(solution)/shard_map/ppermute | solution.py:17
  247.0 136.7 %collective-permute-start.17 = (bf16[1,1024,128]{2,1,0:T(8,128)(2,1)S(1)}, bf16[1,1024,128]{2,1,0:T(8,128)(2,1)}, u32[]{:S(2)}, u32[]{:S(2)}) collective-permute-start(bf16[1,1024,128]{2,1,0:T(8,128)(2,1)S(1)} %bitcast.266), channel_id=1, source_target_pairs={{2,0},{4,2},{6,4},{8,6},{10,8},{12,10},{14,12},{16,14},{18,16},{20... | collective-permute-start | bytes 786440 | tf_op jit(solution)/shard_map/ppermute | solution.py:19
  266.0 252.7 %all-reduce.8.cloned.1.call-start = ((), (), s32[]{:S(2)}) async-start(), calls=%async_computation.2 | async-start | bytes 131072 | tf_op jit(solution)/shard_map/psum | solution.py:86
  380.9 4.5 copy-start.4
Sparse Core Ops, SparseCore 0:
  241.2 24.6 all-reduce.3
  269.4 86.1 all-reduce.5
Sparse Core Ops, SparseCore 1:
  398.3 120.4 all-reduce.7
